TPU v7x, 32 devices: a whole 2x2x4 slice. The times are simulated.
32 devices in a mesh: row: 4 (over z), col: 2 (over x), depth: 4 (over y, core).
Axes of the slice: x: 2, y: 2, z: 4, core: 2. Of those that a mesh axis runs over, the one named last changes fastest.
Arguments:
- eri_tiles: bfloat16 [48, 64, 128, 128], P('row', ('col', 'depth')), may hold values from -0.0625 to 0.0625
- screen: int32 [48, 64], P('row', ('col', 'depth')), may hold values from 0 to 1, as said below
- density_bra: bfloat16 [6144, 256], P('row', 'col'), may hold values from -6 to 6
- density_ket: bfloat16 [8192, 256], P(('col', 'depth'), 'row'), may hold values from -6 to 6
Outputs:
- coulomb_bra: float32 [6144, 256], P('row', 'col')
- coulomb_ket: float32 [8192, 256], P(('col', 'depth'), 'row')
Inputs may be any that keep to these rules, and one draw needn't show every extreme that they name: `screen`: in each device's block of 12 x 8 tiles (aligned blocks), between 16 and 64 tiles are significant; some block has exactly 64.
All inputs are finite; a program needn't handle non-finite values.
Results may differ from a plain program's by a relative error of at most 0.005.
Values may be sent and summed in bfloat16 or wider, within the bound.
A program may use at most 64 MiB of HBM per device.

v0:
```python
import functools

import jax
import jax.numpy as jnp
from jax import lax
from jax.experimental import pallas as pl
from jax.experimental.pallas import tpu as pltpu
from jax.sharding import PartitionSpec as P

MESH = pl.DeviceIdType.MESH
F32 = jnp.float32


def kernel(
    sizes, eri, screen, dbra, dket, out_b, out_k,
    scr, traw, tmat, kbuf, bbuf, kpart, k_rx, bp, d1_rx, x_rx, y_rx, fin,
    local_sem, ks_send, ks_recv, b_send, b_recv, kr_send, kr_recv, bp_send, bp_recv,
):
    R, C, Dp = sizes
    per = R // C
    G = Dp // 2
    r, c, d = lax.axis_index("row"), lax.axis_index("col"), lax.axis_index("depth")
    h = d % 2
    g = d // 2
    sib = {"depth": d + 1 - 2 * h}
    up, down = {"row": r + 1}, {"row": r - 1}
    A, B, PS = eri.shape[0], eri.shape[1], eri.shape[2]
    rows, cols = tmat.shape
    dk = kbuf.shape[2]
    H = kbuf.shape[1]
    part = cols // H
    db = bbuf.shape[3]
    pending = []

    def send(src, dst, ssem, rsem, dev, cond=None):
        def make():
            return pltpu.make_async_remote_copy(
                src_ref=src, dst_ref=dst, send_sem=ssem, recv_sem=rsem,
                device_id=dev, device_id_type=MESH)

        def start():
            make().start()

        if cond is None:
            start()
        else:
            pl.when(cond)(start)
        pending.append((cond, lambda: make().wait_send()))

    def recv(dst, ssem, rsem, cond=None):
        def go():
            pltpu.make_async_remote_copy(
                src_ref=dst, dst_ref=dst, send_sem=ssem, recv_sem=rsem,
                device_id=sib, device_id_type=MESH).wait_recv()
        if cond is None:
            go()
        else:
            pl.when(cond)(go)

    half = rows // 2
    loads = [
        pltpu.make_async_copy(dbra.at[pl.ds(0, half)], bbuf.at[c, 0], local_sem.at[0]),
        pltpu.make_async_copy(dbra.at[pl.ds(half, half)], bbuf.at[c, 1], local_sem.at[1]),
        pltpu.make_async_copy(eri, traw, local_sem.at[2]),
        pltpu.make_async_copy(screen, scr, local_sem.at[3 + H]),
    ]
    kloads = [
        pltpu.make_async_copy(dket.at[:, pl.ds(u * part, part)], kbuf.at[r, u], local_sem.at[3 + u])
        for u in range(H)
    ]
    for one in kloads:
        one.start()
    for one in loads:
        one.start()

    bar = pltpu.get_barrier_semaphore()

    def hello(dev):
        pl.semaphore_signal(bar, inc=1, device_id=dev, device_id_type=MESH)

    pl.when(r > 0)(lambda: hello(down))
    pl.when(r < R - 1)(lambda: hello(up))
    for o in range(1, C):
        hello({"col": (c + o) % C})
    hello(sib)
    for o in range(1, G):
        hello({"depth": (d + 2 * o) % Dp})
    peers = C + G - 1 + jnp.where(r > 0, 1, 0) + jnp.where(r < R - 1, 1, 0)
    pl.semaphore_wait(bar, peers)

    def ket_send(s, u, dirn, cond):
        send(kbuf.at[s, u], kbuf.at[s, u], ks_send.at[s, dirn, u], ks_recv.at[s, u],
             up if dirn else down, cond)

    for u in range(H):
        kloads[u].wait()
        ket_send(r, u, 0, r > 0)
        ket_send(r, u, 1, r < R - 1)
    loads[0].wait()
    loads[1].wait()
    for o in range(1, C):
        send(bbuf.at[c, h], bbuf.at[c, h], b_send.at[o], b_recv.at[0, c], {"col": (c + o) % C})
    loads[2].wait()
    loads[3].wait()

    for a in range(A):
        for b in range(B):
            keep = scr[b, a] > 0
            tile = traw[a, b]
            tmat[a * PS:(a + 1) * PS, b * PS:(b + 1) * PS] = jnp.where(keep, tile, jnp.zeros_like(tile))

    def ket_block(cb):
        x = bbuf[cb].reshape(rows, db)
        res = lax.dot_general(x, tmat[...], (((0,), (0,)), ((), ())), preferred_element_type=F32)
        for j in range(per):
            for u in range(H):
                kpart[cb * per + j, u] = res[j * dk:(j + 1) * dk, u * part:(u + 1) * part]

    def sum_send(t, u, dirn, cond):
        send(kpart.at[t, u], k_rx.at[dirn, t, u], kr_send.at[dirn, t, u], kr_recv.at[dirn, t, u],
             {"row": r - 1 + 2 * dirn}, cond)

    def sum_recv(t, u, dirn):
        recv(k_rx.at[dirn, t, u], kr_send.at[dirn, t, u], kr_recv.at[dirn, t, u])

    def ket_ends(cb):
        for j in range(per):
            t = cb * per + j
            for u in range(H):
                sum_send(t, u, 0, (r == R - 1) & (t < r))
        for j in reversed(range(per)):
            t = cb * per + j
            for u in range(H):
                sum_send(t, u, 1, (r == 0) & (t > r))

    first = (c * 2) // C

    def ket_forward(late, k):
        dirn = 1 - first if late else first
        t = jnp.where(dirn == 0, k, R - 1 - k)
        cond = jnp.where(dirn == 0, (r < R - 1) & (t < r), (r > 0) & (t > r))
        for u in range(H):
            def go():
                sum_recv(t, u, dirn)
                kpart[t, u] = kpart[t, u] + k_rx[dirn, t, u]
            pl.when(cond)(go)
            sum_send(t, u, dirn, cond)

    def ket_final():
        for u in range(H):
            at = slice(u * part, (u + 1) * part)
            out_k[:, at] = kpart[r, u]

            def take(dirn):
                sum_recv(r, u, dirn)
                out_k[:, at] += k_rx[dirn, r, u]
            pl.when(r < R - 1)(lambda: take(0))
            pl.when(r > 0)(lambda: take(1))

    near = jnp.minimum(r, R - 1 - r)

    def slot(i):
        k = (i + 1) // 2
        inner = r - k if i % 2 == 1 else r + k
        outer = jnp.where(r > R - 1 - r, r - (i - near), r + (i - near))
        return jnp.where(i <= 2 * near, inner, outer)

    order = [slot(i) for i in range(R)]

    def bra_a(i, close=None):
        s = order[i]
        here = None if close is None else (near >= 1 if close else near < 1)

        def gate(x):
            return x if here is None else x & here
        for u in range(H):
            recv(kbuf.at[s, u], ks_send.at[s, 0, u], ks_recv.at[s, u], here)
            ket_send(s, u, 0, gate((s > r) & (r > 0)))
            ket_send(s, u, 1, gate((s < r) & (r < R - 1)))

    def bra_dot(i):
        s = order[i]
        res = sum(
            lax.dot_general(kbuf[s, u], tmat[:, u * part:(u + 1) * part], (((1,), (1,)), ((), ())),
                            preferred_element_type=F32)
            for u in range(H))
        bp[s, 0] = res[:, :half]
        bp[s, 1] = res[:, half:]
        send(bp.at[s, 1 - h], d1_rx.at[s], bp_send.at[0, s], bp_recv.at[0, s], sib)

    def bra_b(i):
        s = order[i]
        cs, j = s // per, s % per
        recv(d1_rx.at[s], bp_send.at[0, s], bp_recv.at[0, s])
        bp[s, h] = bp[s, h] + d1_rx[s]
        send(bp.at[s, h], x_rx.at[c, j], bp_send.at[1, s], bp_recv.at[1, c * per + j], {"col": cs}, cs != c)

    def bra_c(i):
        s = order[i]
        cs, j = s // per, s % per

        def go():
            total = bp[s, h]
            for o in range(1, C):
                p = (c + o) % C
                recv(x_rx.at[p, j], bp_send.at[1, s], bp_recv.at[1, p * per + j])
                total = total + x_rx[p, j]
            y_rx[j, g] = total
        pl.when(cs == c)(go)
        for o in range(1, G):
            send(y_rx.at[j, g], y_rx.at[j, g], bp_send.at[1 + o, s], bp_recv.at[2, j * G + g],
                 {"depth": (d + 2 * o) % Dp}, cs == c)

    def bra_d(i):
        s = order[i]
        cs, j = s // per, s % per

        def go():
            for o in range(1, G):
                q = (g + o) % G
                recv(y_rx.at[j, q], bp_send.at[2, s], bp_recv.at[2, j * G + q])
            total = y_rx[j, 0]
            for q in range(1, G):
                total = total + y_rx[j, q]
            fin[j, h] = total
        pl.when(cs == c)(go)
        send(fin.at[j, h], fin.at[j, h], bp_send.at[G + 1, s], bp_recv.at[3, j], sib, cs == c)

    def bra_e():
        for j in range(per):
            recv(fin.at[j, 1 - h], bp_send.at[G + 1, 0], bp_recv.at[3, j])
            out_b[j * dk:(j + 1) * dk, :half] = fin[j, 0]
            out_b[j * dk:(j + 1) * dk, half:] = fin[j, 1]

    others = [(c + o) % C for o in range(1, C)]
    ket_block(c)
    ket_ends(c)
    bra_dot(0)
    bra_a(1)
    bra_b(0)
    bra_dot(1)
    for p in others:
        recv(bbuf.at[p, h], b_send.at[0], b_recv.at[0, p])
        send(bbuf.at[p, h], bbuf.at[p, h], b_send.at[C + p], b_recv.at[1, p], sib)
    bra_a(2, True)
    bra_b(1)
    for p in others:
        recv(bbuf.at[p, 1 - h], b_send.at[0], b_recv.at[1, p])
        ket_block(p)
        ket_ends(p)
    bra_a(2, False)
    bra_dot(2)
    bra_a(3, True)
    ket_forward(False, 0)
    bra_c(0)
    bra_b(2)
    bra_a(3, False)
    bra_dot(3)
    ket_forward(False, 1)
    bra_c(1)
    bra_b(3)
    for i in range(4, R):
        bra_a(i)
        bra_dot(i)
        bra_b(i)
    bra_c(2)
    ket_forward(True, 0)
    bra_c(3)
    bra_d(0)
    for k in range(2, R - 1):
        ket_forward(False, k)
        ket_forward(True, k - 1)
    bra_d(1)
    for i in range(4, R):
        bra_c(i)
    ket_forward(True, R - 2)
    for i in range(2, R):
        bra_d(i)
    bra_e()
    ket_final()

    for cond, wait in pending:
        if cond is None:
            wait()
        else:
            pl.when(cond)(wait)


def body(sizes, eri_tiles, screen, density_bra, density_ket):
    R, C, Dp = sizes
    A, B, PS, _ = eri_tiles.shape
    rows, cols = A * PS, B * PS
    db, dk = density_bra.shape[1], density_ket.shape[1]
    per, G, half, H = R // C, Dp // 2, rows // 2, 2
    DMA = pltpu.SemaphoreType.DMA
    hbm = pl.BlockSpec(memory_space=pltpu.HBM)
    vm = pl.BlockSpec(memory_space=pltpu.VMEM)
    out_b, out_k = pl.pallas_call(
        functools.partial(kernel, sizes),
        out_shape=(jax.ShapeDtypeStruct((db, rows), F32), jax.ShapeDtypeStruct((dk, cols), F32)),
        in_specs=[hbm, hbm, hbm, hbm],
        out_specs=(vm, vm),
        scratch_shapes=[
            pltpu.SMEM((B, A), jnp.int32),
            pltpu.VMEM((A, B, PS, PS), jnp.bfloat16),
            pltpu.VMEM((rows, cols), jnp.bfloat16),
            pltpu.VMEM((R, H, dk, cols // H), jnp.bfloat16),
            pltpu.VMEM((C, 2, half, db), jnp.bfloat16),
            pltpu.VMEM((R, H, dk, cols // H), F32),
            pltpu.VMEM((2, R, H, dk, cols // H), F32),
            pltpu.VMEM((R, 2, dk, half), F32),
            pltpu.VMEM((R, dk, half), F32),
            pltpu.VMEM((C, per, dk, half), F32),
            pltpu.VMEM((per, G, dk, half), F32),
            pltpu.VMEM((per, 2, dk, half), F32),
            DMA((4 + H,)),
            DMA((R, 2, H)), DMA((R, H)),
            DMA((2 * C,)), DMA((2, C)),
            DMA((2, R, H)), DMA((2, R, H)),
            DMA((G + 2, R)), DMA((4, max(R, per * G))),
        ],
        compiler_params=pltpu.CompilerParams(
            collective_id=0, has_side_effects=True, vmem_limit_bytes=28 * 1024 * 1024),
    )(*(pltpu.with_memory_space_constraint(x, pltpu.HBM) for x in (eri_tiles, screen.T, density_bra, density_ket.T)))
    return out_b.T, out_k.T


def solution(mesh):
    sizes = (mesh.shape["row"], mesh.shape["col"], mesh.shape["depth"])
    return jax.shard_map(
        functools.partial(body, sizes),
        mesh=mesh,
        in_specs=(
            P("row", ("col", "depth"), None, None),
            P("row", ("col", "depth")),
            P("row", "col"),
            P(("col", "depth"), "row"),
        ),
        out_specs=(P("row", "col"), P(("col", "depth"), "row")),
        check_vma=False,
    )
```

profile of v0, /device:TPU:11, one launch (start us, length us, event | category | flops | bytes accessed | tf_op | source)
XLA Modules:
  0.0 41.1 jit_solution(13825379414920572574)
XLA Ops:
  0.6 38.6 %shard_map.59 = (f32[128,1536]{1,0:T(8,128)S(1)}, f32[64,1024]{1,0:T(8,128)S(1)}) custom-call(bf16[12,8,128,128]{3,2,1,0:T(8,128)(2,1)} %eri.1, s32[8,12]{1,0:T(8,128)} %bitcast.7, bf16[1536,128]{1,0:T(8,128)(2,1)} %dbra.1, bf16[64,1024]{1,0:T(8,128)(2,1)} %bitcast.6), custom_call_target="tpu_custom_call" | custom-call | tf_op jit(solution)/shard_map/pallas_call | solution.py:298
  39.3 1.1 %copy.6 = f32[1536,128]{1,0:T(8,128)} copy(f32[1536,128]{0,1:T(8,128)S(1)} %bitcast.4) | data formatting | bytes 1572864
  40.4 0.7 %copy.8 = f32[1024,64]{0,1:T(8,128)} copy(f32[1024,64]{0,1:T(8,128)S(1)} %bitcast.5) | data formatting | bytes 524288
where the time goes:
time: 41.3 us; the launch traced here: 41.1 us
  Pallas kernels  38.6 us (93%)
  local copies, waits for them, and re-layouts  1.85 us (4%)
  between operations  0.64 us (2%)
    pallas_call x1, Pallas kernels, body(): pl.pallas_call(functools.partial(kernel, sizes), out_shape=(jax.ShapeDtyp...  38.6 us
    unnamed x2, local copies, waits for them, and re-layouts  1.85 us

commit v1 on v0

v1 whole, which is shorter than its diff:
```python
import functools

import jax
import jax.numpy as jnp
from jax import lax
from jax.experimental import pallas as pl
from jax.experimental.pallas import tpu as pltpu
from jax.sharding import PartitionSpec as P

MESH = pl.DeviceIdType.MESH
F32 = jnp.float32
KP = 2
SP = 4
BP = 2


def kernel(
    sizes, eri, screen, dbra, dket, out_b, out_k,
    scr, traw, tmat, kbuf, bbuf, kpart, k_rx, bp, d1_rx, x_rx, y_rx, fin,
    local_sem, ks_send, ks_recv, b_send, b_recv, kr_send, kr_recv,
    d1_send, d1_recv, x_send, x_recv, y_send, y_recv, f_send, f_recv,
):
    R, C, Dp = sizes
    per = R // C
    G = Dp // 2
    r, c, d = lax.axis_index("row"), lax.axis_index("col"), lax.axis_index("depth")
    h = d % 2
    g = d // 2
    sib = {"depth": d + 1 - 2 * h}
    A, B, PS = eri.shape[0], eri.shape[1], eri.shape[2]
    rows, cols = tmat.shape
    dk, kw = kbuf.shape[2], kbuf.shape[3]
    sw = kpart.shape[3]
    db = bbuf.shape[3]
    half = rows // 2
    bw = half // BP
    near = jnp.minimum(r, R - 1 - r)
    edge, inside = near == 0, near > 0
    pending = {"first": [], "last": []}

    def when(cond, fn):
        if cond is None:
            fn()
        else:
            pl.when(cond)(fn)

    def remote(src, dst, ssem, rsem, dev):
        return pltpu.make_async_remote_copy(
            src_ref=src, dst_ref=dst, send_sem=ssem, recv_sem=rsem, device_id=dev, device_id_type=MESH)

    def sent(cond, src, ssem, group="first"):
        pending[group].append((cond, lambda: remote(src, src, ssem, ssem, sib).wait_send()))

    def recv(dst, rsem):
        remote(dst, dst, rsem, rsem, sib).wait_recv()

    def flush(group):
        for cond, wait in pending[group]:
            when(cond, wait)

    loads = [
        pltpu.make_async_copy(dbra.at[pl.ds(0, half)], bbuf.at[c, 0], local_sem.at[0]),
        pltpu.make_async_copy(dbra.at[pl.ds(half, half)], bbuf.at[c, 1], local_sem.at[1]),
        pltpu.make_async_copy(eri, traw, local_sem.at[2]),
        pltpu.make_async_copy(screen, scr, local_sem.at[3 + KP]),
    ]
    kloads = [
        pltpu.make_async_copy(dket.at[:, pl.ds(u * kw, kw)], kbuf.at[r, u], local_sem.at[3 + u])
        for u in range(KP)
    ]
    for one in kloads:
        one.start()
    for one in loads:
        one.start()

    bar = pltpu.get_barrier_semaphore()

    def hello(dev):
        pl.semaphore_signal(bar, inc=1, device_id=dev, device_id_type=MESH)

    pl.when(r > 0)(lambda: hello({"row": r - 1}))
    pl.when(r < R - 1)(lambda: hello({"row": r + 1}))
    for o in range(1, C):
        hello({"col": (c + o) % C})
    hello(sib)
    for o in range(1, G):
        hello({"depth": (d + 2 * o) % Dp})
    pl.semaphore_wait(bar, C + G - 1 + jnp.where(r > 0, 1, 0) + jnp.where(r < R - 1, 1, 0))

    def ket_send(s, u, dirn, cond):
        pl.when(cond)(lambda: remote(
            kbuf.at[s, u], kbuf.at[s, u], ks_send.at[s, dirn], ks_recv.at[s, u], {"row": r - 1 + 2 * dirn}).start())

    for u in range(KP):
        kloads[u].wait()
        ket_send(r, u, 0, r > 0)
        ket_send(r, u, 1, r < R - 1)
    loads[0].wait()
    loads[1].wait()
    for o in range(1, C):
        remote(bbuf.at[c, h], bbuf.at[c, h], b_send.at[o], b_recv.at[0, c], {"col": (c + o) % C}).start()
        sent(None, bbuf.at[c, h], b_send.at[o])
    for dirn in range(2):
        sent((r < R - 1) if dirn else (r > 0), kbuf.at[r], ks_send.at[r, dirn])
    loads[2].wait()
    loads[3].wait()

    for a in range(A):
        for b in range(B):
            keep = scr[b, a] > 0
            tile = traw[a, b]
            tmat[a * PS:(a + 1) * PS, b * PS:(b + 1) * PS] = jnp.where(keep, tile, jnp.zeros_like(tile))

    def ket_block(cb):
        x = bbuf[cb].reshape(rows, db)
        res = lax.dot_general(x, tmat[...], (((0,), (0,)), ((), ())), preferred_element_type=F32)
        for j in range(per):
            for u in range(SP):
                kpart[cb * per + j, u] = res[j * dk:(j + 1) * dk, u * sw:(u + 1) * sw]

    def sum_send(t, u, dirn):
        remote(kpart.at[t, u], k_rx.at[dirn, t, u], kr_send.at[t], kr_recv.at[dirn, t, u],
               {"row": r - 1 + 2 * dirn}).start()

    mine = r // per == c

    def ket_ends(cb, which):
        for dirn in range(2):
            for j in range(per):
                t = cb * per + (per - 1 - j if dirn else j)
                go = (r == 0) & (t > r) if dirn else (r == R - 1) & (t < r)
                for u in range(SP):
                    ok = go
                    if which == "early" and u == SP - 1:
                        ok = go & jnp.logical_not(mine)
                    elif which == "rest":
                        if u < SP - 1:
                            continue
                        ok = go & mine
                    pl.when(ok)(functools.partial(sum_send, t, u, dirn))

    first = (c * 2) // C

    def flow(late, slot):
        dirn = 1 - first if late else first
        hop = jnp.where(dirn == 0, R - 1 - r, r)
        p = slot - 2 * (hop - 1) + (0 if late else 2)
        k, u = p // SP, p % SP
        t = jnp.where(dirn == 0, k, R - 1 - k)
        onward = R - 1 - hop

        def go():
            recv(k_rx.at[dirn, t, u], kr_recv.at[dirn, t, u])
            kpart[t, u] = kpart[t, u] + k_rx[dirn, t, u]
            pl.when(k < onward)(lambda: sum_send(t, u, dirn))
        pl.when((hop >= 1) & (p >= 0) & (k <= onward))(go)

    def slot_of(i):
        k = (i + 1) // 2
        inner = r - k if i % 2 == 1 else r + k
        inner = jnp.where(2 * r < R, 2 * r - inner, inner)
        outer = jnp.where(r > R - 1 - r, r - (i - near), r + (i - near))
        return jnp.where(i <= 2 * near, inner, outer)

    order = [slot_of(i) for i in range(R)]

    def ket_take(i, us, cond=None):
        s = order[i]

        def go():
            for u in us:
                recv(kbuf.at[s, u], ks_recv.at[s, u])
                ket_send(s, u, 0, (s > r) & (r > 0))
                ket_send(s, u, 1, (s < r) & (r < R - 1))
        when(cond, go)
        if us[-1] == KP - 1:
            def both(x):
                return x if cond is None else x & cond
            sent(both((s > r) & (r > 0)), kbuf.at[s], ks_send.at[s, 0])
            sent(both((s < r) & (r < R - 1)), kbuf.at[s], ks_send.at[s, 1])

    def bra_dot(i):
        s = order[i]
        res = sum(
            lax.dot_general(kbuf[s, u], tmat[:, u * kw:(u + 1) * kw], (((1,), (1,)), ((), ())),
                            preferred_element_type=F32)
            for u in range(KP))
        for q in range(BP):
            bp[s, 0, q] = res[:, q * bw:(q + 1) * bw]
            bp[s, 1, q] = res[:, half + q * bw:half + (q + 1) * bw]
        remote(bp.at[s, 1 - h], d1_rx.at[s], d1_send.at[s], d1_recv.at[s], sib).start()
        sent(None, bp.at[s, 1 - h], d1_send.at[s])

    def bra_b(i, cond=None):
        s = order[i]
        cs, j = s // per, s % per

        def go():
            recv(d1_rx.at[s], d1_recv.at[s])
            for q in range(BP):
                bp[s, h, q] = bp[s, h, q] + d1_rx[s, q]
                pl.when(cs != c)(lambda: remote(
                    bp.at[s, h, q], x_rx.at[c, j, q], x_send.at[s], x_recv.at[c, j, q], {"col": cs}).start())
        when(cond, go)
        sent(cs != c if cond is None else (cs != c) & cond, bp.at[s, h], x_send.at[s], "last")

    def bra_c(i, q, cond):
        s = order[i]
        cs, j = s // per, s % per

        def go():
            total = bp[s, h, q]
            for o in range(1, C):
                p = (c + o) % C
                recv(x_rx.at[p, j, q], x_recv.at[p, j, q])
                total = total + x_rx[p, j, q]
            y_rx[j, g, q] = total
            for o in range(1, G):
                remote(y_rx.at[j, g, q], y_rx.at[j, g, q], y_send.at[o, j], y_recv.at[j, g, q],
                       {"depth": (d + 2 * o) % Dp}).start()
        pl.when((cs == c) & cond)(go)

    def out_at(j, q, side):
        return pl.ds(pl.multiple_of(j * dk, 8), dk), pl.ds(pl.multiple_of(side * half + q * bw, 128), bw)

    def bra_d(i, q, cond):
        s = order[i]
        cs, j = s // per, s % per

        def go():
            for o in range(1, G):
                p = (g + o) % G
                recv(y_rx.at[j, p, q], y_recv.at[j, p, q])
            total = y_rx[j, 0, q]
            for p in range(1, G):
                total = total + y_rx[j, p, q]
            fin[j, q] = total
            at = out_at(j, q, h)
            remote(fin.at[j, q], out_b.at[at], f_send.at[j], f_recv.at[j, q], sib).start()
            out_b[at] = total
        pl.when((cs == c) & cond)(go)

    def bra_e():
        for j in range(per):
            for q in range(BP):
                recv(fin.at[j, q], f_recv.at[j, q])

    tail = []
    for late in (False, True):
        for slot in range(-2, (R - 1) * SP + 2 * R - 4):
            tail.append((10.5 + 1.4 * slot, functools.partial(flow, late, slot)))
    start_e = {0: 10.0, 1: 14.2, 2: 15.0, 3: 19.2}
    start_m = {0: 10.0, 2: 14.2, 1: 12.0, 3: 16.2}
    for i in range(R):
        for q in range(BP):
            for cond, table in ((edge, start_e), (inside, start_m)):
                at = table.get(i, 19.2 + 4.2 * (i - 3)) + 2.1 * q
                tail.append((at, functools.partial(bra_c, i, q, cond)))
                tail.append((at + 3.1, functools.partial(bra_d, i, q, cond)))
    tail.sort(key=lambda x: x[0])

    def run_tail(until):
        while tail and tail[0][0] < until:
            tail.pop(0)[1]()

    others = [(c + o) % C for o in range(1, C)]
    every = range(KP)
    ket_block(c)
    ket_ends(c, "early")
    bra_dot(0)
    ket_take(1, every, edge)
    for u in every:
        for i in (1, 2):
            ket_take(i, [u], inside)
    bra_dot(1)
    bra_b(0)
    for p in others:
        recv(bbuf.at[p, h], b_recv.at[0, p])
        remote(bbuf.at[p, h], bbuf.at[p, h], b_send.at[C + p], b_recv.at[1, p], sib).start()
        sent(None, bbuf.at[p, h], b_send.at[C + p])
    ket_take(3, [0], inside)
    bra_b(1)
    for p in others:
        recv(bbuf.at[p, 1 - h], b_recv.at[1, p])
        ket_block(p)
        ket_ends(p, "all")
    ket_ends(c, "rest")
    ket_take(3, list(range(1, KP)), inside)
    ket_take(2, every, edge)
    bra_dot(2)
    run_tail(10.0)
    ket_take(3, every, edge)
    bra_dot(3)
    bra_b(2)
    for i in range(4, R):
        ket_take(i, every)
        bra_dot(i)
        bra_b(i)
    run_tail(13.0)
    bra_b(3)
    run_tail(16.5)
    flush("first")
    run_tail(21.5)
    flush("last")
    pending["last"].clear()
    run_tail(1e9)
    bra_e()
    for u in range(SP):
        out_k[:, u * sw:(u + 1) * sw] = kpart[r, u]
    for t in range(R):
        sent(t != r, kpart.at[t], kr_send.at[t], "last")
    for j in range(per):
        for o in range(1, G):
            sent(None, y_rx.at[j, g], y_send.at[o, j], "last")
        sent(None, fin.at[j], f_send.at[j], "last")
    flush("last")


def body(sizes, eri_tiles, screen, density_bra, density_ket):
    R, C, Dp = sizes
    A, B, PS, _ = eri_tiles.shape
    rows, cols = A * PS, B * PS
    db, dk = density_bra.shape[1], density_ket.shape[1]
    per, G, half = R // C, Dp // 2, rows // 2
    DMA = pltpu.SemaphoreType.DMA
    hbm = pl.BlockSpec(memory_space=pltpu.HBM)
    vm = pl.BlockSpec(memory_space=pltpu.VMEM)
    piece = (dk, half // BP)
    out_b, out_k = pl.pallas_call(
        functools.partial(kernel, sizes),
        out_shape=(jax.ShapeDtypeStruct((db, rows), F32), jax.ShapeDtypeStruct((dk, cols), F32)),
        in_specs=[hbm, hbm, hbm, hbm],
        out_specs=(vm, vm),
        scratch_shapes=[
            pltpu.SMEM((B, A), jnp.int32),
            pltpu.VMEM((A, B, PS, PS), jnp.bfloat16),
            pltpu.VMEM((rows, cols), jnp.bfloat16),
            pltpu.VMEM((R, KP, dk, cols // KP), jnp.bfloat16),
            pltpu.VMEM((C, 2, half, db), jnp.bfloat16),
            pltpu.VMEM((R, SP, dk, cols // SP), F32),
            pltpu.VMEM((2, R, SP, dk, cols // SP), F32),
            pltpu.VMEM((R, 2, BP, *piece), F32),
            pltpu.VMEM((R, BP, *piece), F32),
            pltpu.VMEM((C, per, BP, *piece), F32),
            pltpu.VMEM((per, G, BP, *piece), F32),
            pltpu.VMEM((per, BP, *piece), F32),
            DMA((4 + KP,)),
            DMA((R, 2)), DMA((R, KP)),
            DMA((2 * C,)), DMA((2, C)),
            DMA((R,)), DMA((2, R, SP)),
            DMA((R,)), DMA((R,)),
            DMA((R,)), DMA((C, per, BP)),
            DMA((G, per)), DMA((per, G, BP)),
            DMA((per,)), DMA((per, BP)),
        ],
        compiler_params=pltpu.CompilerParams(
            collective_id=0, has_side_effects=True, vmem_limit_bytes=28 * 1024 * 1024),
    )(*(pltpu.with_memory_space_constraint(x, pltpu.HBM) for x in (eri_tiles, screen.T, density_bra, density_ket.T)))
    return out_b.T, out_k.T


def solution(mesh):
    sizes = (mesh.shape["row"], mesh.shape["col"], mesh.shape["depth"])
    return jax.shard_map(
        functools.partial(body, sizes),
        mesh=mesh,
        in_specs=(
            P("row", ("col", "depth"), None, None),
            P("row", ("col", "depth")),
            P("row", "col"),
            P(("col", "depth"), "row"),
        ),
        out_specs=(P("row", "col"), P(("col", "depth"), "row")),
        check_vma=False,
    )
```

time: 41.3 us -> 36.1 us (0.87)
  the two profiles are of different devices: /device:TPU:11 before, /device:TPU:3 now
where the time goes in v1:
time: 36.1 us; the launch traced here: 35.8 us
  Pallas kernels  33.3 us (92%)
  local copies, waits for them, and re-layouts  1.85 us (5%)
  between operations  0.64 us (2%)
    pallas_call x1, Pallas kernels, body(): pl.pallas_call(functools.partial(kernel, sizes), out_shape=(jax.ShapeDtyp...  33.3 us
    unnamed x2, local copies, waits for them, and re-layouts  1.85 us

profile of v1, /device:TPU:3, one launch (start us, length us, event | category | flops | bytes accessed | tf_op | source)
XLA Modules:
  0.0 35.8 jit_solution(18019377849150095944)
XLA Ops:
  0.6 33.3 %shard_map.59 = (f32[128,1536]{1,0:T(8,128)S(1)}, f32[64,1024]{1,0:T(8,128)S(1)}) custom-call(bf16[12,8,128,128]{3,2,1,0:T(8,128)(2,1)} %eri.1, s32[8,12]{1,0:T(8,128)} %bitcast.7, bf16[1536,128]{1,0:T(8,128)(2,1)} %dbra.1, bf16[64,1024]{1,0:T(8,128)(2,1)} %bitcast.6), custom_call_target="tpu_custom_call" | custom-call | tf_op jit(solution)/shard_map/pallas_call | solution.py:329
  33.9 1.1 %copy.6 = f32[1536,128]{1,0:T(8,128)} copy(f32[1536,128]{0,1:T(8,128)S(1)} %bitcast.4) | data formatting | bytes 1572864
  35.1 0.7 %copy.8 = f32[1024,64]{0,1:T(8,128)} copy(f32[1024,64]{0,1:T(8,128)S(1)} %bitcast.5) | data formatting | bytes 524288

commit v2 on v1

v2 whole, which is shorter than its diff:
```python
import functools

import jax
import jax.numpy as jnp
from jax import lax
from jax.experimental import pallas as pl
from jax.experimental.pallas import tpu as pltpu
from jax.sharding import PartitionSpec as P

MESH = pl.DeviceIdType.MESH
F32 = jnp.float32
KP = 2
SP = 4
HOPS = (5, 3)
BP = 3


def kernel(
    sizes, eri, screen, dbra, dket, out_b, out_k,
    scr, traw, tmat, kbuf, bbuf, kpart, k_rx, bp, d1_rx, x_rx, y_rx, fin,
    local_sem, send_sem, ks_recv, b_recv, kr_recv, d1_recv, x_recv, y_recv, f_recv,
):
    R, C, Dp = sizes
    per = R // C
    G = Dp // 2
    r, c, d = lax.axis_index("row"), lax.axis_index("col"), lax.axis_index("depth")
    h = d % 2
    g = d // 2
    sib = {"depth": d + 1 - 2 * h}
    A, B, PS = eri.shape[0], eri.shape[1], eri.shape[2]
    rows, cols = tmat.shape
    dk, kw = kbuf.shape[2], kbuf.shape[3]
    sw = kpart.shape[3]
    db = bbuf.shape[3]
    half = rows // 2
    bw = half // BP
    near = jnp.minimum(r, R - 1 - r)
    pending = {"first": [], "last": []}

    def when(cond, fn):
        if cond is None:
            fn()
        else:
            pl.when(cond)(fn)

    def remote(src, dst, rsem, dev):
        return pltpu.make_async_remote_copy(
            src_ref=src, dst_ref=dst, send_sem=send_sem, recv_sem=rsem, device_id=dev, device_id_type=MESH)

    def sent(cond, src, group="first"):
        pending[group].append((cond, lambda: remote(src, src, send_sem, sib).wait_send()))

    def recv(dst, rsem):
        remote(dst, dst, rsem, sib).wait_recv()

    def flush(group):
        for cond, wait in pending[group]:
            when(cond, wait)

    loads = [
        pltpu.make_async_copy(dbra.at[pl.ds(0, half)], bbuf.at[c, 0], local_sem.at[0]),
        pltpu.make_async_copy(dbra.at[pl.ds(half, half)], bbuf.at[c, 1], local_sem.at[1]),
        pltpu.make_async_copy(eri, traw, local_sem.at[2]),
        pltpu.make_async_copy(screen, scr, local_sem.at[3 + KP]),
    ]
    kloads = [
        pltpu.make_async_copy(dket.at[:, pl.ds(u * kw, kw)], kbuf.at[r, u], local_sem.at[3 + u])
        for u in range(KP)
    ]
    for one in kloads:
        one.start()
    for one in loads:
        one.start()

    bar = pltpu.get_barrier_semaphore()

    def hello(dev):
        pl.semaphore_signal(bar, inc=1, device_id=dev, device_id_type=MESH)

    pl.when(r > 0)(lambda: hello({"row": r - 1}))
    pl.when(r < R - 1)(lambda: hello({"row": r + 1}))
    for o in range(1, C):
        hello({"col": (c + o) % C})
    hello(sib)
    for o in range(1, G):
        hello({"depth": (d + 2 * o) % Dp})
    pl.semaphore_wait(bar, C + G - 1 + jnp.where(r > 0, 1, 0) + jnp.where(r < R - 1, 1, 0))

    def ket_send(s, u, dirn, cond):
        pl.when(cond)(lambda: remote(
            kbuf.at[s, u], kbuf.at[s, u], ks_recv.at[s, u], {"row": r - 1 + 2 * dirn}).start())

    for u in range(KP):
        kloads[u].wait()
        ket_send(r, u, 0, r > 0)
        ket_send(r, u, 1, r < R - 1)
    loads[0].wait()
    loads[1].wait()
    for o in range(1, C):
        remote(bbuf.at[c, h], bbuf.at[c, h], b_recv.at[0, C - 1 - o], {"col": (c + o) % C}).start()
        sent(None, bbuf.at[c, h])
    for dirn in range(2):
        sent((r < R - 1) if dirn else (r > 0), kbuf.at[r])
    loads[2].wait()
    loads[3].wait()

    for a in range(A):
        for b in range(B):
            keep = scr[b, a] > 0
            tile = traw[a, b]
            tmat[a * PS:(a + 1) * PS, b * PS:(b + 1) * PS] = jnp.where(keep, tile, jnp.zeros_like(tile))

    def ket_block(cb):
        x = bbuf[cb].reshape(rows, db)
        res = lax.dot_general(x, tmat[...], (((0,), (0,)), ((), ())), preferred_element_type=F32)
        for j in range(per):
            for u in range(SP):
                kpart[cb * per + j, u] = res[j * dk:(j + 1) * dk, u * sw:(u + 1) * sw]

    def sum_send(t, u, dirn):
        remote(kpart.at[t, u], k_rx.at[dirn, t, u], kr_recv.at[t + dirn, u],
               {"row": r - 1 + 2 * dirn}).start()

    mine = r // per == c

    def ket_ends(cb, pieces, only=None):
        for dirn in range(2):
            for j in range(per):
                t = cb * per + (per - 1 - j if dirn else j)
                go = (r == 0) & (t > r) if dirn else (r == R - 1) & (t < r)
                for u in pieces:
                    ok = go if only is None or u < SP - 1 and not only else go & (mine if only else ~mine)
                    pl.when(ok)(functools.partial(sum_send, t, u, dirn))

    first = (c * 2) // C

    def flow(late, p):
        dirn = 1 - first if late else first
        hop = jnp.where(dirn == 0, R - 1 - r, r)

        def go(p):
            k, u = p // SP, p % SP
            t = jnp.where(dirn == 0, k, R - 1 - k)
            recv(k_rx.at[dirn, t, u], kr_recv.at[t + dirn, u])
            kpart[t, u] = kpart[t, u] + k_rx[dirn, t, u]
            pl.when(k < R - 1 - hop)(lambda: sum_send(t, u, dirn))
        p = p - HOPS[late] * (hop - 1)
        pl.when((hop >= 1) & (p >= 0) & (p < (R - hop) * SP))(lambda: go(p))

    def slot_of(i):
        k = (i + 1) // 2
        inner = r - k if i % 2 == 1 else r + k
        inner = jnp.where(2 * r < R, 2 * r - inner, inner)
        outer = jnp.where(r > R - 1 - r, r - (i - near), r + (i - near))
        return jnp.where(i <= 2 * near, inner, outer)

    order = [slot_of(i) for i in range(R)]

    def ket_take(i, u):
        s = order[i]
        recv(kbuf.at[s, u], ks_recv.at[s, u])
        for dirn, on in ((0, (s > r) & (r > 0)), (1, (s < r) & (r < R - 1))):
            ket_send(s, u, dirn, on)
            if u == KP - 1:
                sent(on, kbuf.at[s])

    def bra_dot(i, u):
        s = order[i]
        for side, other in ((1 - h, True), (h, False)):
            part = tmat[pl.ds(pl.multiple_of(side * half, 128), half), u * kw:(u + 1) * kw]
            res = lax.dot_general(kbuf[s, u], part, (((1,), (1,)), ((), ())), preferred_element_type=F32)
            for q in range(BP):
                term = res[:, q * bw:(q + 1) * bw]
                bp[s, side, q] = term if u == 0 else bp[s, side, q] + term
            if other and u == KP - 1:
                for q in range(BP):
                    remote(bp.at[s, side, q], d1_rx.at[s, q], d1_recv.at[s, q], sib).start()
        if u == KP - 1:
            sent(None, bp.at[s, 1 - h])

    def bra_b(i):
        s = order[i]
        cs, j = s // per, s % per
        for q in range(BP):
            recv(d1_rx.at[s, q], d1_recv.at[s, q])
            bp[s, h, q] = bp[s, h, q] + d1_rx[s, q]
            pl.when(cs != c)(lambda: remote(
                bp.at[s, h, q], x_rx.at[c, j, q], x_recv.at[(c - cs + C - 1) % C, j, q], {"col": cs}).start())
        sent(cs != c, bp.at[s, h], "last")

    def bra_c(i, q):
        s = order[i]
        cs, j = s // per, s % per

        def go():
            total = bp[s, h, q]
            for o in range(1, C):
                p = (c + o) % C
                recv(x_rx.at[p, j, q], x_recv.at[o - 1, j, q])
                total = total + x_rx[p, j, q]
            y_rx[j, g, q] = total
            for o in range(1, G):
                remote(y_rx.at[j, g, q], y_rx.at[j, g, q], y_recv.at[j, G - 1 - o, q],
                       {"depth": (d + 2 * o) % Dp}).start()
        pl.when(cs == c)(go)

    def out_at(j, q, side):
        return pl.ds(pl.multiple_of(j * dk, 8), dk), pl.ds(pl.multiple_of(side * half + q * bw, 128), bw)

    def bra_d(i, q):
        s = order[i]
        cs, j = s // per, s % per

        def go():
            for o in range(1, G):
                p = (g + o) % G
                recv(y_rx.at[j, p, q], y_recv.at[j, o - 1, q])
            total = y_rx[j, 0, q]
            for p in range(1, G):
                total = total + y_rx[j, p, q]
            fin[j, q] = total
            at = out_at(j, q, h)
            remote(fin.at[j, q], out_b.at[at], f_recv, sib).start()
            out_b[at] = total
        pl.when(cs == c)(go)

    def bra_e():
        recv(fin, f_recv)

    others = [(c + o) % C for o in range(1, C)]

    def bra_forward():
        for o, p in enumerate(others):
            recv(bbuf.at[p, h], b_recv.at[0, o])
            remote(bbuf.at[p, h], bbuf.at[p, h], b_recv.at[1, o], sib).start()
            sent(None, bbuf.at[p, h])

    def ket_others():
        for o, p in enumerate(others):
            recv(bbuf.at[p, 1 - h], b_recv.at[1, o])
            ket_block(p)
            ket_ends(p, range(SP))

    def start_edge():
        ket_ends(c, range(SP), False)
        for u in range(KP):
            bra_dot(0, u)
        for u in range(KP):
            ket_take(1, u)
            bra_dot(1, u)
        bra_forward()
        bra_b(0)
        ket_others()
        ket_ends(c, [SP - 1], True)
        bra_b(1)
        for u in range(KP):
            ket_take(2, u)
            bra_dot(2, u)
        for i in range(3, R):
            bra_b(i - 1)
            for u in range(KP):
                ket_take(i, u)
                bra_dot(i, u)
        return R - 1

    def start_inside():
        for u in range(KP):
            bra_dot(0, u)
        for u in range(KP):
            ket_take(1, u)
            ket_take(2, u)
            bra_dot(1, u)
        bra_b(0)
        for u in range(KP):
            bra_dot(2, u)
        bra_forward()
        for u in range(KP):
            ket_take(3, u)
            bra_dot(3, u)
            if u == 0:
                bra_b(1)
        ket_others()
        bra_b(2)
        for i in range(4, R):
            for u in range(KP):
                ket_take(i, u)
                bra_dot(i, u)
            bra_b(i - 1)
        return R - 1

    def finish(kind, last):
        tail = [(16.1 if kind == "edge" else 12.1, bra_b, (last,))]
        for late in (False, True):
            lag = HOPS[late]
            if kind == "edge":
                steps = range(lag * (R - 2), lag * (R - 2) + SP)
            else:
                steps = range(max((R - hop) * SP + lag * (hop - 1) for hop in range(1, R - 1)))
            for p in steps:
                tail.append(((13.0 if late else 8.9) + 1.4 * p, flow, (late, p)))
        start = {0: 11.3, 1: 15.5, 2: 16.1, 3: 20.3} if kind == "edge" else {0: 11.2, 2: 15.2, 1: 13.4, 3: 17.6}
        for i in range(R):
            for q in range(BP):
                at = start.get(i, 20.3 + 4.2 * (i - 3)) + 4.2 / BP * q
                tail.append((at, bra_c, (i, q)))
                tail.append((at + 2.2 + 4.2 / BP, bra_d, (i, q)))
        tail.sort(key=lambda x: x[0])
        first_done = last_done = False
        for at, fn, args in tail:
            if at > 19 and not first_done:
                flush("first")
                first_done = True
            if at > 23.6 and not last_done:
                flush("last")
                last_done = True
            fn(*args)
        bra_e()
        for u in range(SP):
            out_k[:, u * sw:(u + 1) * sw] = kpart[r, u]
        pending["last"].clear()
        for t in range(R):
            sent(t != r, kpart.at[t], "last")
        for j in range(per):
            for o in range(1, G):
                sent(None, y_rx.at[j, g], "last")
            sent(None, fin.at[j], "last")
        flush("last")

    ket_block(c)
    front = list(pending["first"])

    def run(kind):
        pending["first"], pending["last"] = list(front), []
        finish(kind, start_edge() if kind == "edge" else start_inside())

    pl.when(near == 0)(lambda: run("edge"))
    pl.when(near > 0)(lambda: run("inside"))


def body(sizes, eri_tiles, screen, density_bra, density_ket):
    R, C, Dp = sizes
    A, B, PS, _ = eri_tiles.shape
    rows, cols = A * PS, B * PS
    db, dk = density_bra.shape[1], density_ket.shape[1]
    per, G, half = R // C, Dp // 2, rows // 2
    DMA = pltpu.SemaphoreType.DMA
    hbm = pl.BlockSpec(memory_space=pltpu.HBM)
    vm = pl.BlockSpec(memory_space=pltpu.VMEM)
    piece = (dk, half // BP)
    out_b, out_k = pl.pallas_call(
        functools.partial(kernel, sizes),
        out_shape=(jax.ShapeDtypeStruct((db, rows), F32), jax.ShapeDtypeStruct((dk, cols), F32)),
        in_specs=[hbm, hbm, hbm, hbm],
        out_specs=(vm, vm),
        scratch_shapes=[
            pltpu.SMEM((B, A), jnp.int32),
            pltpu.VMEM((A, B, PS, PS), jnp.bfloat16),
            pltpu.VMEM((rows, cols), jnp.bfloat16),
            pltpu.VMEM((R, KP, dk, cols // KP), jnp.bfloat16),
            pltpu.VMEM((C, 2, half, db), jnp.bfloat16),
            pltpu.VMEM((R, SP, dk, cols // SP), F32),
            pltpu.VMEM((2, R, SP, dk, cols // SP), F32),
            pltpu.VMEM((R, 2, BP, *piece), F32),
            pltpu.VMEM((R, BP, *piece), F32),
            pltpu.VMEM((C, per, BP, *piece), F32),
            pltpu.VMEM((per, G, BP, *piece), F32),
            pltpu.VMEM((per, BP, *piece), F32),
            DMA((4 + KP,)), DMA, DMA((R, KP)), DMA((2, C - 1)), DMA((R + 1, SP)),
            DMA((R, BP)), DMA((C - 1, per, BP)), DMA((per, G - 1, BP)), DMA,
        ],
        compiler_params=pltpu.CompilerParams(
            collective_id=0, has_side_effects=True, vmem_limit_bytes=28 * 1024 * 1024),
    )(*(pltpu.with_memory_space_constraint(x, pltpu.HBM) for x in (eri_tiles, screen.T, density_bra, density_ket.T)))
    return out_b.T, out_k.T


def solution(mesh):
    sizes = (mesh.shape["row"], mesh.shape["col"], mesh.shape["depth"])
    return jax.shard_map(
        functools.partial(body, sizes),
        mesh=mesh,
        in_specs=(
            P("row", ("col", "depth"), None, None),
            P("row", ("col", "depth")),
            P("row", "col"),
            P(("col", "depth"), "row"),
        ),
        out_specs=(P("row", "col"), P(("col", "depth"), "row")),
        check_vma=False,
    )
```

time: 36.1 us -> 31.7 us (0.88)
  Pallas kernels: 33.3 us -> 29.1 us
    pallas_call x1, Pallas kernels: 33.3 us -> 29.1 us  [body(): pl.pallas_call(functools.partial(kernel, sizes), out_shape=(jax.ShapeDtyp...]
where the time goes in v2:
time: 31.7 us; the launch traced here: 31.6 us
  Pallas kernels  29.1 us (92%)
  local copies, waits for them, and re-layouts  1.85 us (6%)
  between operations  0.64 us (2%)
    pallas_call x1, Pallas kernels, body(): pl.pallas_call(functools.partial(kernel, sizes), out_shape=(jax.ShapeDtyp...  29.1 us
    unnamed x2, local copies, waits for them, and re-layouts  1.85 us

profile of v2, /device:TPU:3, one launch (start us, length us, event | category | flops | bytes accessed | tf_op | source)
XLA Modules:
  0.0 31.6 jit_solution(12993438759439001754)
XLA Ops:
  0.6 29.1 %shard_map.59 = (f32[128,1536]{1,0:T(8,128)S(1)}, f32[64,1024]{1,0:T(8,128)S(1)}) custom-call(bf16[12,8,128,128]{3,2,1,0:T(8,128)(2,1)} %eri.1, s32[8,12]{1,0:T(8,128)} %bitcast.7, bf16[1536,128]{1,0:T(8,128)(2,1)} %dbra.1, bf16[64,1024]{1,0:T(8,128)(2,1)} %bitcast.6), custom_call_target="tpu_custom_call" | custom-call | tf_op jit(solution)/shard_map/pallas_call | solution.py:350
  29.7 1.1 %copy.6 = f32[1536,128]{1,0:T(8,128)} copy(f32[1536,128]{0,1:T(8,128)S(1)} %bitcast.4) | data formatting | bytes 1572864
  30.9 0.7 %copy.8 = f32[1024,64]{0,1:T(8,128)} copy(f32[1024,64]{0,1:T(8,128)S(1)} %bitcast.5) | data formatting | bytes 524288

commit v3 on v2

--- a/solution.py
+++ b/solution.py
@@ -9,15 +9,37 @@
 
 MESH = pl.DeviceIdType.MESH
 F32 = jnp.float32
-KP = 2
+BF16 = jnp.bfloat16
+STEPS = 7 * 2.0**8
+KP = 4
+KD = 2
 SP = 4
-HOPS = (5, 3)
+HOPS = (8, 4)
+STORES = 4
 BP = 3
+
+
+def pack(ref, v):
+    w = v.shape[1]
+    top = v.astype(BF16)
+    near = top.astype(F32)
+    rest = jnp.round((v - near) / jnp.where(near == 0, 1.0, near) * STEPS)
+    ref[:, :w] = top
+    ref[:, w:] = (rest[:, :w // 2] * 16 + rest[:, w // 2:]).astype(BF16)
+
+
+def unpack(ref):
+    w = ref.shape[1] * 2 // 3
+    near = ref[:, :w].astype(F32)
+    both = ref[:, w:].astype(F32)
+    high = jnp.round(both * (1 / 16))
+    rest = jnp.concatenate([high, both - high * 16], 1)
+    return near + near * rest * (1 / STEPS)
 
 
 def kernel(
     sizes, eri, screen, dbra, dket, out_b, out_k,
-    scr, traw, tmat, kbuf, bbuf, kpart, k_rx, bp, d1_rx, x_rx, y_rx, fin,
+    scr, traw, tmat, kbuf, bbuf, kpart, k_tx, k_rx, bp, d1_rx, x_tx, x_rx, y_rx, fin,
     local_sem, send_sem, ks_recv, b_recv, kr_recv, d1_recv, x_recv, y_recv, f_recv,
 ):
     R, C, Dp = sizes
@@ -28,7 +50,7 @@
     g = d // 2
     sib = {"depth": d + 1 - 2 * h}
     A, B, PS = eri.shape[0], eri.shape[1], eri.shape[2]
-    rows, cols = tmat.shape
+    rows, cols = A * PS, B * PS
     dk, kw = kbuf.shape[2], kbuf.shape[3]
     sw = kpart.shape[3]
     db = bbuf.shape[3]
@@ -108,18 +130,19 @@
         for b in range(B):
             keep = scr[b, a] > 0
             tile = traw[a, b]
-            tmat[a * PS:(a + 1) * PS, b * PS:(b + 1) * PS] = jnp.where(keep, tile, jnp.zeros_like(tile))
+            at = a % (A // 2) * PS
+            tmat[a // (A // 2), at:at + PS, b * PS:(b + 1) * PS] = jnp.where(keep, tile, jnp.zeros_like(tile))
 
     def ket_block(cb):
         x = bbuf[cb].reshape(rows, db)
-        res = lax.dot_general(x, tmat[...], (((0,), (0,)), ((), ())), preferred_element_type=F32)
+        res = lax.dot_general(x, tmat[...].reshape(rows, cols), (((0,), (0,)), ((), ())), preferred_element_type=F32)
         for j in range(per):
             for u in range(SP):
                 kpart[cb * per + j, u] = res[j * dk:(j + 1) * dk, u * sw:(u + 1) * sw]
 
     def sum_send(t, u, dirn):
-        remote(kpart.at[t, u], k_rx.at[dirn, t, u], kr_recv.at[t + dirn, u],
-               {"row": r - 1 + 2 * dirn}).start()
+        pack(k_tx.at[t, u], kpart[t, u])
+        remote(k_tx.at[t, u], k_rx.at[dirn, t, u], kr_recv.at[t + dirn, u], {"row": r - 1 + 2 * dirn}).start()
 
     mine = r // per == c
 
@@ -142,7 +165,7 @@
             k, u = p // SP, p % SP
             t = jnp.where(dirn == 0, k, R - 1 - k)
             recv(k_rx.at[dirn, t, u], kr_recv.at[t + dirn, u])
-            kpart[t, u] = kpart[t, u] + k_rx[dirn, t, u]
+            kpart[t, u] = kpart[t, u] + unpack(k_rx.at[dirn, t, u])
             pl.when(k < R - 1 - hop)(lambda: sum_send(t, u, dirn))
         p = p - HOPS[late] * (hop - 1)
         pl.when((hop >= 1) & (p >= 0) & (p < (R - hop) * SP))(lambda: go(p))
@@ -167,15 +190,16 @@
     def bra_dot(i, u):
         s = order[i]
         for side, other in ((1 - h, True), (h, False)):
-            part = tmat[pl.ds(pl.multiple_of(side * half, 128), half), u * kw:(u + 1) * kw]
-            res = lax.dot_general(kbuf[s, u], part, (((1,), (1,)), ((), ())), preferred_element_type=F32)
+            part = tmat[side, :, u * kw * KP // KD:(u + 1) * kw * KP // KD]
+            left = jnp.concatenate([kbuf[s, u * KP // KD + v] for v in range(KP // KD)], 1)
+            res = lax.dot_general(left, part, (((1,), (1,)), ((), ())), preferred_element_type=F32)
             for q in range(BP):
                 term = res[:, q * bw:(q + 1) * bw]
                 bp[s, side, q] = term if u == 0 else bp[s, side, q] + term
-            if other and u == KP - 1:
+            if other and u == KD - 1:
                 for q in range(BP):
                     remote(bp.at[s, side, q], d1_rx.at[s, q], d1_recv.at[s, q], sib).start()
-        if u == KP - 1:
+        if u == KD - 1:
             sent(None, bp.at[s, 1 - h])
 
     def bra_b(i):
@@ -183,10 +207,14 @@
         cs, j = s // per, s % per
         for q in range(BP):
             recv(d1_rx.at[s, q], d1_recv.at[s, q])
-            bp[s, h, q] = bp[s, h, q] + d1_rx[s, q]
-            pl.when(cs != c)(lambda: remote(
-                bp.at[s, h, q], x_rx.at[c, j, q], x_recv.at[(c - cs + C - 1) % C, j, q], {"col": cs}).start())
-        sent(cs != c, bp.at[s, h], "last")
+            total = bp[s, h, q] + d1_rx[s, q]
+            bp[s, h, q] = total
+
+            def go():
+                pack(x_tx.at[s, q], total)
+                remote(x_tx.at[s, q], x_rx.at[c, j, q], x_recv.at[(c - cs + C - 1) % C, j, q], {"col": cs}).start()
+            pl.when(cs != c)(go)
+        sent(cs != c, x_tx.at[s], "last")
 
     def bra_c(i, q):
         s = order[i]
@@ -197,8 +225,8 @@
             for o in range(1, C):
                 p = (c + o) % C
                 recv(x_rx.at[p, j, q], x_recv.at[o - 1, j, q])
-                total = total + x_rx[p, j, q]
-            y_rx[j, g, q] = total
+                total = total + unpack(x_rx.at[p, j, q])
+            pack(y_rx.at[j, g, q], total)
             for o in range(1, G):
                 remote(y_rx.at[j, g, q], y_rx.at[j, g, q], y_recv.at[j, G - 1 - o, q],
                        {"depth": (d + 2 * o) % Dp}).start()
@@ -215,9 +243,9 @@
             for o in range(1, G):
                 p = (g + o) % G
                 recv(y_rx.at[j, p, q], y_recv.at[j, o - 1, q])
-            total = y_rx[j, 0, q]
+            total = unpack(y_rx.at[j, 0, q])
             for p in range(1, G):
-                total = total + y_rx[j, p, q]
+                total = total + unpack(y_rx.at[j, p, q])
             fin[j, q] = total
             at = out_at(j, q, h)
             remote(fin.at[j, q], out_b.at[at], f_recv, sib).start()
@@ -241,55 +269,54 @@
             ket_block(p)
             ket_ends(p, range(SP))
 
+    def take_dot(i, u, *more):
+        for v in range(KP // KD):
+            for k in (i, *more):
+                ket_take(k, u * KP // KD + v)
+        bra_dot(i, u)
+
     def start_edge():
         ket_ends(c, range(SP), False)
-        for u in range(KP):
+        for u in range(KD):
             bra_dot(0, u)
-        for u in range(KP):
-            ket_take(1, u)
-            bra_dot(1, u)
+        for u in range(KD):
+            take_dot(1, u)
         bra_forward()
         bra_b(0)
         ket_others()
         ket_ends(c, [SP - 1], True)
         bra_b(1)
-        for u in range(KP):
-            ket_take(2, u)
-            bra_dot(2, u)
+        for u in range(KD):
+            take_dot(2, u)
         for i in range(3, R):
             bra_b(i - 1)
-            for u in range(KP):
-                ket_take(i, u)
-                bra_dot(i, u)
+            for u in range(KD):
+                take_dot(i, u)
         return R - 1
 
     def start_inside():
-        for u in range(KP):
+        for u in range(KD):
             bra_dot(0, u)
-        for u in range(KP):
-            ket_take(1, u)
-            ket_take(2, u)
-            bra_dot(1, u)
+        for u in range(KD):
+            take_dot(1, u, 2)
         bra_b(0)
-        for u in range(KP):
+        for u in range(KD):
             bra_dot(2, u)
         bra_forward()
-        for u in range(KP):
-            ket_take(3, u)
-            bra_dot(3, u)
+        for u in range(KD):
+            take_dot(3, u)
             if u == 0:
                 bra_b(1)
         ket_others()
         bra_b(2)
         for i in range(4, R):
-            for u in range(KP):
-                ket_take(i, u)
-                bra_dot(i, u)
+            for u in range(KD):
+                take_dot(i, u)
             bra_b(i - 1)
         return R - 1
 
     def finish(kind, last):
-        tail = [(16.1 if kind == "edge" else 12.1, bra_b, (last,))]
+        tail = [(10.0 if kind == "edge" else 12.1, bra_b, (last,))]
         for late in (False, True):
             lag = HOPS[late]
             if kind == "edge":
@@ -297,13 +324,13 @@
             else:
                 steps = range(max((R - hop) * SP + lag * (hop - 1) for hop in range(1, R - 1)))
             for p in steps:
-                tail.append(((13.0 if late else 8.9) + 1.4 * p, flow, (late, p)))
-        start = {0: 11.3, 1: 15.5, 2: 16.1, 3: 20.3} if kind == "edge" else {0: 11.2, 2: 15.2, 1: 13.4, 3: 17.6}
+                tail.append(((13.5 if late else 8.5) + 1.05 * p, flow, (late, p)))
+        start = {0: 11.3, 1: 14.5, 2: 15.6, 3: 20.0} if kind == "edge" else {0: 11.2, 2: 16.0, 1: 13.4, 3: 16.6}
         for i in range(R):
             for q in range(BP):
-                at = start.get(i, 20.3 + 4.2 * (i - 3)) + 4.2 / BP * q
+                at = start.get(i, 20.0 + 4.2 * (i - 3)) + 3.2 / BP * q
                 tail.append((at, bra_c, (i, q)))
-                tail.append((at + 2.2 + 4.2 / BP, bra_d, (i, q)))
+                tail.append((at + 2.5 + 3.2 / BP, bra_d, (i, q)))
         tail.sort(key=lambda x: x[0])
         first_done = last_done = False
         for at, fn, args in tail:
@@ -319,7 +346,7 @@
             out_k[:, u * sw:(u + 1) * sw] = kpart[r, u]
         pending["last"].clear()
         for t in range(R):
-            sent(t != r, kpart.at[t], "last")
+            sent(t != r, k_tx.at[t], "last")
         for j in range(per):
             for o in range(1, G):
                 sent(None, y_rx.at[j, g], "last")
@@ -335,6 +362,20 @@
 
     pl.when(near == 0)(lambda: run("edge"))
     pl.when(near > 0)(lambda: run("inside"))
+
+
+def store(bra_t, ket_t, bra, ket, turned, sem):
+    kets = pltpu.make_async_copy(ket_t, ket, sem.at[0])
+    kets.start()
+    size = turned.shape[0] // STORES
+    copies = []
+    for i in range(STORES):
+        at = pl.ds(i * size, size)
+        turned[at] = bra_t[:, at].T
+        copies.append(pltpu.make_async_copy(turned.at[at], bra.at[at], sem.at[1 + i]))
+        copies[-1].start()
+    for one in [kets, *copies]:
+        one.wait()
 
 
 def body(sizes, eri_tiles, screen, density_bra, density_ket):
@@ -346,7 +387,7 @@
     DMA = pltpu.SemaphoreType.DMA
     hbm = pl.BlockSpec(memory_space=pltpu.HBM)
     vm = pl.BlockSpec(memory_space=pltpu.VMEM)
-    piece = (dk, half // BP)
+    piece, coded = (dk, half // BP), (dk, half // BP * 3 // 2)
     out_b, out_k = pl.pallas_call(
         functools.partial(kernel, sizes),
         out_shape=(jax.ShapeDtypeStruct((db, rows), F32), jax.ShapeDtypeStruct((dk, cols), F32)),
@@ -354,16 +395,18 @@
         out_specs=(vm, vm),
         scratch_shapes=[
             pltpu.SMEM((B, A), jnp.int32),
-            pltpu.VMEM((A, B, PS, PS), jnp.bfloat16),
-            pltpu.VMEM((rows, cols), jnp.bfloat16),
-            pltpu.VMEM((R, KP, dk, cols // KP), jnp.bfloat16),
-            pltpu.VMEM((C, 2, half, db), jnp.bfloat16),
+            pltpu.VMEM((A, B, PS, PS), BF16),
+            pltpu.VMEM((2, half, cols), BF16),
+            pltpu.VMEM((R, KP, dk, cols // KP), BF16),
+            pltpu.VMEM((C, 2, half, db), BF16),
             pltpu.VMEM((R, SP, dk, cols // SP), F32),
-            pltpu.VMEM((2, R, SP, dk, cols // SP), F32),
+            pltpu.VMEM((R, SP, dk, cols // SP * 3 // 2), BF16),
+            pltpu.VMEM((2, R, SP, dk, cols // SP * 3 // 2), BF16),
             pltpu.VMEM((R, 2, BP, *piece), F32),
             pltpu.VMEM((R, BP, *piece), F32),
-            pltpu.VMEM((C, per, BP, *piece), F32),
-            pltpu.VMEM((per, G, BP, *piece), F32),
+            pltpu.VMEM((R, BP, *coded), BF16),
+            pltpu.VMEM((C, per, BP, *coded), BF16),
+            pltpu.VMEM((per, G, BP, *coded), BF16),
             pltpu.VMEM((per, BP, *piece), F32),
             DMA((4 + KP,)), DMA, DMA((R, KP)), DMA((2, C - 1)), DMA((R + 1, SP)),
             DMA((R, BP)), DMA((C - 1, per, BP)), DMA((per, G - 1, BP)), DMA,
@@ -371,7 +414,15 @@
         compiler_params=pltpu.CompilerParams(
             collective_id=0, has_side_effects=True, vmem_limit_bytes=28 * 1024 * 1024),
     )(*(pltpu.with_memory_space_constraint(x, pltpu.HBM) for x in (eri_tiles, screen.T, density_bra, density_ket.T)))
-    return out_b.T, out_k.T
+    bra, ket = pl.pallas_call(
+        store,
+        out_shape=(jax.ShapeDtypeStruct((rows, db), F32), jax.ShapeDtypeStruct((dk, cols), F32)),
+        in_specs=[vm, vm],
+        out_specs=(hbm, hbm),
+        scratch_shapes=[pltpu.VMEM((rows, db), F32), DMA((1 + STORES,))],
+        compiler_params=pltpu.CompilerParams(vmem_limit_bytes=4 * 1024 * 1024),
+    )(out_b, out_k)
+    return bra, ket.T
 
 
 def solution(mesh):

time: 31.7 us -> 29.3 us (0.924)
  the two profiles are of different devices: /device:TPU:3 before, /device:TPU:0 now
where the time goes in v3:
time: 29.3 us; the launch traced here: 29.1 us
  Pallas kernels  28.3 us (97%)
  between operations  0.82 us (3%)
    pallas_call x1, Pallas kernels, body(): pl.pallas_call(functools.partial(kernel, sizes), out_shape=(jax.ShapeDtyp...  27.3 us
    pallas_call x1, Pallas kernels, body(): pl.pallas_call(store, out_shape=(jax.ShapeDtypeStruct((rows, db), F32), j...  1.05 us

profile of v3, /device:TPU:0, one launch (start us, length us, event | category | flops | bytes accessed | tf_op | source)
XLA Modules:
  0.0 29.1 jit_solution(17027198770694039711)
XLA Ops:
  0.6 27.3 %shard_map.59 = (f32[128,1536]{1,0:T(8,128)S(1)}, f32[64,1024]{1,0:T(8,128)S(1)}) custom-call(bf16[12,8,128,128]{3,2,1,0:T(8,128)(2,1)} %eri.1, s32[8,12]{1,0:T(8,128)} %bitcast.4, bf16[1536,128]{1,0:T(8,128)(2,1)} %dbra.1, bf16[64,1024]{1,0:T(8,128)(2,1)} %bitcast.3), custom_call_target="tpu_custom_call" | custom-call | tf_op jit(solution)/shard_map/pallas_call | solution.py:391
  27.9 1.0 %shard_map.60 = (f32[1536,128]{1,0:T(8,128)}, f32[64,1024]{1,0:T(8,128)}) custom-call(f32[128,1536]{1,0:T(8,128)S(1)} %get-tuple-element.6.bra_t, f32[64,1024]{1,0:T(8,128)S(1)} %get-tuple-element.7.ket_t), custom_call_target="tpu_custom_call" | custom-call | tf_op jit(solution)/shard_map/pallas_call | solution.py:417

commit v4 on v3

--- a/solution.py
+++ b/solution.py
@@ -12,9 +12,8 @@
 BF16 = jnp.bfloat16
 STEPS = 7 * 2.0**8
 KP = 4
-KD = 2
 SP = 4
-HOPS = (8, 4)
+HOPS = (6, 4)
 STORES = 4
 BP = 3
 
@@ -81,19 +80,14 @@
 
     loads = [
         pltpu.make_async_copy(dbra.at[pl.ds(0, half)], bbuf.at[c, 0], local_sem.at[0]),
-        pltpu.make_async_copy(dbra.at[pl.ds(half, half)], bbuf.at[c, 1], local_sem.at[1]),
-        pltpu.make_async_copy(eri, traw, local_sem.at[2]),
-        pltpu.make_async_copy(screen, scr, local_sem.at[3 + KP]),
+        pltpu.make_async_copy(dbra.at[pl.ds(half, half)], bbuf.at[c, 1], local_sem.at[0]),
+        pltpu.make_async_copy(eri, traw, local_sem.at[1]),
+        pltpu.make_async_copy(screen, scr, local_sem.at[2]),
     ]
     kloads = [
-        pltpu.make_async_copy(dket.at[:, pl.ds(u * kw, kw)], kbuf.at[r, u], local_sem.at[3 + u])
+        pltpu.make_async_copy(dket.at[:, pl.ds(u * kw, kw)], kbuf.at[r, u], local_sem.at[3])
         for u in range(KP)
     ]
-    for one in kloads:
-        one.start()
-    for one in loads:
-        one.start()
-
     bar = pltpu.get_barrier_semaphore()
 
     def hello(dev):
@@ -106,18 +100,21 @@
     hello(sib)
     for o in range(1, G):
         hello({"depth": (d + 2 * o) % Dp})
+    for one in kloads:
+        one.start()
+    for one in loads:
+        one.start()
     pl.semaphore_wait(bar, C + G - 1 + jnp.where(r > 0, 1, 0) + jnp.where(r < R - 1, 1, 0))
 
     def ket_send(s, u, dirn, cond):
         pl.when(cond)(lambda: remote(
             kbuf.at[s, u], kbuf.at[s, u], ks_recv.at[s, u], {"row": r - 1 + 2 * dirn}).start())
 
+    pltpu.make_async_copy(kbuf.at[r], kbuf.at[r], local_sem.at[3]).wait()
     for u in range(KP):
-        kloads[u].wait()
         ket_send(r, u, 0, r > 0)
         ket_send(r, u, 1, r < R - 1)
-    loads[0].wait()
-    loads[1].wait()
+    pltpu.make_async_copy(bbuf.at[c], bbuf.at[c], local_sem.at[0]).wait()
     for o in range(1, C):
         remote(bbuf.at[c, h], bbuf.at[c, h], b_recv.at[0, C - 1 - o], {"col": (c + o) % C}).start()
         sent(None, bbuf.at[c, h])
@@ -130,12 +127,11 @@
         for b in range(B):
             keep = scr[b, a] > 0
             tile = traw[a, b]
-            at = a % (A // 2) * PS
-            tmat[a // (A // 2), at:at + PS, b * PS:(b + 1) * PS] = jnp.where(keep, tile, jnp.zeros_like(tile))
+            tmat[a * PS:(a + 1) * PS, b * PS:(b + 1) * PS] = jnp.where(keep, tile, jnp.zeros_like(tile))
 
     def ket_block(cb):
         x = bbuf[cb].reshape(rows, db)
-        res = lax.dot_general(x, tmat[...].reshape(rows, cols), (((0,), (0,)), ((), ())), preferred_element_type=F32)
+        res = lax.dot_general(x, tmat[...], (((0,), (0,)), ((), ())), preferred_element_type=F32)
         for j in range(per):
             for u in range(SP):
                 kpart[cb * per + j, u] = res[j * dk:(j + 1) * dk, u * sw:(u + 1) * sw]
@@ -187,19 +183,17 @@
             if u == KP - 1:
                 sent(on, kbuf.at[s])
 
-    def bra_dot(i, u):
+    def bra_dot(i, lo, hi):
         s = order[i]
-        for side, other in ((1 - h, True), (h, False)):
-            part = tmat[side, :, u * kw * KP // KD:(u + 1) * kw * KP // KD]
-            left = jnp.concatenate([kbuf[s, u * KP // KD + v] for v in range(KP // KD)], 1)
-            res = lax.dot_general(left, part, (((1,), (1,)), ((), ())), preferred_element_type=F32)
-            for q in range(BP):
-                term = res[:, q * bw:(q + 1) * bw]
-                bp[s, side, q] = term if u == 0 else bp[s, side, q] + term
-            if other and u == KD - 1:
-                for q in range(BP):
-                    remote(bp.at[s, side, q], d1_rx.at[s, q], d1_recv.at[s, q], sib).start()
-        if u == KD - 1:
+        left = jnp.concatenate([kbuf[s, u] for u in range(lo, hi)], 1)
+        res = lax.dot_general(left, tmat[:, lo * kw:hi * kw], (((1,), (1,)), ((), ())), preferred_element_type=F32)
+        for q in range(BP):
+            for x in range(2):
+                term = res[:, x * half + q * bw:x * half + (q + 1) * bw]
+                bp[s, x, q] = term if lo == 0 else bp[s, x, q] + term
+            if hi == KP:
+                remote(bp.at[s, 1 - h, q], d1_rx.at[s, q], d1_recv.at[s, q], sib).start()
+        if hi == KP:
             sent(None, bp.at[s, 1 - h])
 
     def bra_b(i):
@@ -269,54 +263,58 @@
             ket_block(p)
             ket_ends(p, range(SP))
 
-    def take_dot(i, u, *more):
-        for v in range(KP // KD):
+    def take_dot(i, lo, hi, *more):
+        for u in range(lo, hi):
             for k in (i, *more):
-                ket_take(k, u * KP // KD + v)
-        bra_dot(i, u)
+                ket_take(k, u)
+        bra_dot(i, lo, hi)
+
+    mid = KP // 2
 
     def start_edge():
         ket_ends(c, range(SP), False)
-        for u in range(KD):
-            bra_dot(0, u)
-        for u in range(KD):
-            take_dot(1, u)
+        bra_dot(0, 0, KP)
+        take_dot(1, 0, mid)
+        take_dot(1, mid, KP)
         bra_forward()
         bra_b(0)
         ket_others()
         ket_ends(c, [SP - 1], True)
         bra_b(1)
-        for u in range(KD):
-            take_dot(2, u)
-        for i in range(3, R):
-            bra_b(i - 1)
-            for u in range(KD):
-                take_dot(i, u)
+        for i in range(2, R):
+            if i > 2:
+                bra_b(i - 1)
+                for q in range(BP):
+                    bra_c(i - 3, q)
+            take_dot(i, 0, mid)
+            take_dot(i, mid, KP - 1)
+            take_dot(i, KP - 1, KP)
+        for q in range(BP):
+            bra_c(R - 2, q)
+        bra_b(R - 1)
+        for q in range(BP):
+            bra_c(R - 3, q)
         return R - 1
 
     def start_inside():
-        for u in range(KD):
-            bra_dot(0, u)
-        for u in range(KD):
-            take_dot(1, u, 2)
+        bra_dot(0, 0, KP)
+        take_dot(1, 0, mid, 2)
+        take_dot(1, mid, KP, 2)
         bra_b(0)
-        for u in range(KD):
-            bra_dot(2, u)
+        bra_dot(2, 0, KP)
         bra_forward()
-        for u in range(KD):
-            take_dot(3, u)
-            if u == 0:
-                bra_b(1)
+        take_dot(3, 0, mid)
+        bra_b(1)
+        take_dot(3, mid, KP)
         ket_others()
         bra_b(2)
         for i in range(4, R):
-            for u in range(KD):
-                take_dot(i, u)
+            take_dot(i, 0, KP)
             bra_b(i - 1)
-        return R - 1
-
-    def finish(kind, last):
-        tail = [(10.0 if kind == "edge" else 12.1, bra_b, (last,))]
+        return 0
+
+    def finish(kind, done):
+        tail = [] if kind == "edge" else [(12.1, bra_b, (R - 1,))]
         for late in (False, True):
             lag = HOPS[late]
             if kind == "edge":
@@ -325,12 +323,16 @@
                 steps = range(max((R - hop) * SP + lag * (hop - 1) for hop in range(1, R - 1)))
             for p in steps:
                 tail.append(((13.5 if late else 8.5) + 1.05 * p, flow, (late, p)))
-        start = {0: 11.3, 1: 14.5, 2: 15.6, 3: 20.0} if kind == "edge" else {0: 11.2, 2: 16.0, 1: 13.4, 3: 16.6}
+        if kind == "edge":
+            when_bra = {0: (12.9, 16.5, 1.0), 1: (15.5, 19.2, 1.0), 2: (15.6, 22.3, 0.1), 3: (19.0, 22.5, 1.05)}
+        else:
+            when_bra = {0: (12.4, 16.5, 0.6), 1: (13.4, 17.1, 1.0), 2: (16.0, 20.7, 0.5), 3: (16.0, 20.1, 1.0)}
         for i in range(R):
+            col_at, depth_at, step = when_bra.get(i, (19.0 + 4 * (i - 3), 22.5 + 4 * (i - 3), 1.05))
             for q in range(BP):
-                at = start.get(i, 20.0 + 4.2 * (i - 3)) + 3.2 / BP * q
-                tail.append((at, bra_c, (i, q)))
-                tail.append((at + 2.5 + 3.2 / BP, bra_d, (i, q)))
+                if i >= done:
+                    tail.append((col_at + step * q, bra_c, (i, q)))
+                tail.append((depth_at + step * q, bra_d, (i, q)))
         tail.sort(key=lambda x: x[0])
         first_done = last_done = False
         for at, fn, args in tail:
@@ -396,7 +398,7 @@
         scratch_shapes=[
             pltpu.SMEM((B, A), jnp.int32),
             pltpu.VMEM((A, B, PS, PS), BF16),
-            pltpu.VMEM((2, half, cols), BF16),
+            pltpu.VMEM((rows, cols), BF16),
             pltpu.VMEM((R, KP, dk, cols // KP), BF16),
             pltpu.VMEM((C, 2, half, db), BF16),
             pltpu.VMEM((R, SP, dk, cols // SP), F32),
@@ -408,7 +410,7 @@
             pltpu.VMEM((C, per, BP, *coded), BF16),
             pltpu.VMEM((per, G, BP, *coded), BF16),
             pltpu.VMEM((per, BP, *piece), F32),
-            DMA((4 + KP,)), DMA, DMA((R, KP)), DMA((2, C - 1)), DMA((R + 1, SP)),
+            DMA((4,)), DMA, DMA((R, KP)), DMA((2, C - 1)), DMA((R + 1, SP)),
             DMA((R, BP)), DMA((C - 1, per, BP)), DMA((per, G - 1, BP)), DMA,
         ],
         compiler_params=pltpu.CompilerParams(

time: 29.3 us -> 27.9 us (0.952)
  the two profiles are of different devices: /device:TPU:0 before, /device:TPU:3 now
where the time goes in v4:
time: 27.9 us; the launch traced here: 27.7 us
  Pallas kernels  26.9 us (96%)
  between operations  0.82 us (3%)
    pallas_call x1, Pallas kernels, body(): pl.pallas_call(functools.partial(kernel, sizes), out_shape=(jax.ShapeDtyp...  25.9 us
    pallas_call x1, Pallas kernels, body(): pl.pallas_call(store, out_shape=(jax.ShapeDtypeStruct((rows, db), F32), j...  1.05 us

profile of v4, /device:TPU:3, one launch (start us, length us, event | category | flops | bytes accessed | tf_op | source)
XLA Modules:
  0.0 27.7 jit_solution(4329490659898087410)
XLA Ops:
  0.6 25.9 %shard_map.59 = (f32[128,1536]{1,0:T(8,128)S(1)}, f32[64,1024]{1,0:T(8,128)S(1)}) custom-call(bf16[12,8,128,128]{3,2,1,0:T(8,128)(2,1)} %eri.1, s32[8,12]{1,0:T(8,128)} %bitcast.4, bf16[1536,128]{1,0:T(8,128)(2,1)} %dbra.1, bf16[64,1024]{1,0:T(8,128)(2,1)} %bitcast.3), custom_call_target="tpu_custom_call" | custom-call | tf_op jit(solution)/shard_map/pallas_call | solution.py:393
  26.5 1.0 %shard_map.60 = (f32[1536,128]{1,0:T(8,128)}, f32[64,1024]{1,0:T(8,128)}) custom-call(f32[128,1536]{1,0:T(8,128)S(1)} %get-tuple-element.6.bra_t, f32[64,1024]{1,0:T(8,128)S(1)} %get-tuple-element.7.ket_t), custom_call_target="tpu_custom_call" | custom-call | tf_op jit(solution)/shard_map/pallas_call | solution.py:419

commit v5 on v4

--- a/solution.py
+++ b/solution.py
@@ -15,7 +15,8 @@
 SP = 4
 HOPS = (6, 4)
 STORES = 4
-BP = 3
+BP = 6
+B0 = 2
 
 
 def pack(ref, v):
@@ -54,7 +55,8 @@
     sw = kpart.shape[3]
     db = bbuf.shape[3]
     half = rows // 2
-    bw = half // BP
+    bw = rows // BP
+    B1 = BP - B0
     near = jnp.minimum(r, R - 1 - r)
     pending = {"first": [], "last": []}
 
@@ -70,6 +72,17 @@
 
     def sent(cond, src, group="first"):
         pending[group].append((cond, lambda: remote(src, src, send_sem, sib).wait_send()))
+
+    def own(q, fn):
+        if q < min(B0, B1):
+            fn()
+        else:
+            pl.when(h == (0 if q < B0 else 1))(fn)
+
+    def sent_own(cond, ref, group="first"):
+        for x, n in ((0, B0), (1, B1)):
+            mine = h == x
+            sent(mine if cond is None else mine & cond, ref.at[pl.ds(0, n)], group)
 
     def recv(dst, rsem):
         remote(dst, dst, rsem, sib).wait_recv()
@@ -187,35 +200,41 @@
         s = order[i]
         left = jnp.concatenate([kbuf[s, u] for u in range(lo, hi)], 1)
         res = lax.dot_general(left, tmat[:, lo * kw:hi * kw], (((1,), (1,)), ((), ())), preferred_element_type=F32)
-        for q in range(BP):
-            for x in range(2):
-                term = res[:, x * half + q * bw:x * half + (q + 1) * bw]
-                bp[s, x, q] = term if lo == 0 else bp[s, x, q] + term
-            if hi == KP:
-                remote(bp.at[s, 1 - h, q], d1_rx.at[s, q], d1_recv.at[s, q], sib).start()
+        for p in range(BP):
+            term = res[:, p * bw:(p + 1) * bw]
+            bp[s, p] = term if lo == 0 else bp[s, p] + term
         if hi == KP:
-            sent(None, bp.at[s, 1 - h])
+            for p in range(BP):
+                q = p if p < B0 else p - B0
+                pl.when(h == (1 if p < B0 else 0))(lambda: remote(
+                    bp.at[s, p], d1_rx.at[s, q], d1_recv.at[s, q], sib).start())
+            sent(h == 1, bp.at[s, pl.ds(0, B0)])
+            sent(h == 0, bp.at[s, pl.ds(B0, B1)])
 
     def bra_b(i):
         s = order[i]
         cs, j = s // per, s % per
-        for q in range(BP):
+
+        def piece(q):
+            p = q + B0 * h
             recv(d1_rx.at[s, q], d1_recv.at[s, q])
-            total = bp[s, h, q] + d1_rx[s, q]
-            bp[s, h, q] = total
+            total = bp[s, p] + d1_rx[s, q]
+            bp[s, p] = total
 
             def go():
                 pack(x_tx.at[s, q], total)
                 remote(x_tx.at[s, q], x_rx.at[c, j, q], x_recv.at[(c - cs + C - 1) % C, j, q], {"col": cs}).start()
             pl.when(cs != c)(go)
-        sent(cs != c, x_tx.at[s], "last")
+        for q in range(max(B0, B1)):
+            own(q, functools.partial(piece, q))
+        sent_own(cs != c, x_tx.at[s], "last")
 
     def bra_c(i, q):
         s = order[i]
         cs, j = s // per, s % per
 
         def go():
-            total = bp[s, h, q]
+            total = bp[s, q + B0 * h]
             for o in range(1, C):
                 p = (c + o) % C
                 recv(x_rx.at[p, j, q], x_recv.at[o - 1, j, q])
@@ -224,10 +243,7 @@
             for o in range(1, G):
                 remote(y_rx.at[j, g, q], y_rx.at[j, g, q], y_recv.at[j, G - 1 - o, q],
                        {"depth": (d + 2 * o) % Dp}).start()
-        pl.when(cs == c)(go)
-
-    def out_at(j, q, side):
-        return pl.ds(pl.multiple_of(j * dk, 8), dk), pl.ds(pl.multiple_of(side * half + q * bw, 128), bw)
+        own(q, lambda: pl.when(cs == c)(go))
 
     def bra_d(i, q):
         s = order[i]
@@ -241,13 +257,14 @@
             for p in range(1, G):
                 total = total + unpack(y_rx.at[j, p, q])
             fin[j, q] = total
-            at = out_at(j, q, h)
+            at = pl.ds(pl.multiple_of(j * dk, 8), dk), pl.ds(pl.multiple_of((q + B0 * h) * bw, 128), bw)
             remote(fin.at[j, q], out_b.at[at], f_recv, sib).start()
             out_b[at] = total
-        pl.when(cs == c)(go)
+        own(q, lambda: pl.when(cs == c)(go))
 
     def bra_e():
-        recv(fin, f_recv)
+        for x, n in ((1, B0), (0, B1)):
+            pl.when(h == x)(lambda: recv(fin.at[:, pl.ds(0, n)], f_recv))
 
     others = [(c + o) % C for o in range(1, C)]
 
@@ -284,15 +301,15 @@
         for i in range(2, R):
             if i > 2:
                 bra_b(i - 1)
-                for q in range(BP):
+                for q in range(max(B0, B1)):
                     bra_c(i - 3, q)
             take_dot(i, 0, mid)
             take_dot(i, mid, KP - 1)
             take_dot(i, KP - 1, KP)
-        for q in range(BP):
+        for q in range(max(B0, B1)):
             bra_c(R - 2, q)
         bra_b(R - 1)
-        for q in range(BP):
+        for q in range(max(B0, B1)):
             bra_c(R - 3, q)
         return R - 1
 
@@ -329,7 +346,7 @@
             when_bra = {0: (12.4, 16.5, 0.6), 1: (13.4, 17.1, 1.0), 2: (16.0, 20.7, 0.5), 3: (16.0, 20.1, 1.0)}
         for i in range(R):
             col_at, depth_at, step = when_bra.get(i, (19.0 + 4 * (i - 3), 22.5 + 4 * (i - 3), 1.05))
-            for q in range(BP):
+            for q in range(max(B0, B1)):
                 if i >= done:
                     tail.append((col_at + step * q, bra_c, (i, q)))
                 tail.append((depth_at + step * q, bra_d, (i, q)))
@@ -351,8 +368,8 @@
             sent(t != r, k_tx.at[t], "last")
         for j in range(per):
             for o in range(1, G):
-                sent(None, y_rx.at[j, g], "last")
-            sent(None, fin.at[j], "last")
+                sent_own(None, y_rx.at[j, g], "last")
+            sent_own(None, fin.at[j], "last")
         flush("last")
 
     ket_block(c)
@@ -389,7 +406,7 @@
     DMA = pltpu.SemaphoreType.DMA
     hbm = pl.BlockSpec(memory_space=pltpu.HBM)
     vm = pl.BlockSpec(memory_space=pltpu.VMEM)
-    piece, coded = (dk, half // BP), (dk, half // BP * 3 // 2)
+    piece, coded, most = (dk, rows // BP), (dk, rows // BP * 3 // 2), max(B0, BP - B0)
     out_b, out_k = pl.pallas_call(
         functools.partial(kernel, sizes),
         out_shape=(jax.ShapeDtypeStruct((db, rows), F32), jax.ShapeDtypeStruct((dk, cols), F32)),
@@ -404,14 +421,14 @@
             pltpu.VMEM((R, SP, dk, cols // SP), F32),
             pltpu.VMEM((R, SP, dk, cols // SP * 3 // 2), BF16),
             pltpu.VMEM((2, R, SP, dk, cols // SP * 3 // 2), BF16),
-            pltpu.VMEM((R, 2, BP, *piece), F32),
             pltpu.VMEM((R, BP, *piece), F32),
-            pltpu.VMEM((R, BP, *coded), BF16),
-            pltpu.VMEM((C, per, BP, *coded), BF16),
-            pltpu.VMEM((per, G, BP, *coded), BF16),
-            pltpu.VMEM((per, BP, *piece), F32),
+            pltpu.VMEM((R, most, *piece), F32),
+            pltpu.VMEM((R, most, *coded), BF16),
+            pltpu.VMEM((C, per, most, *coded), BF16),
+            pltpu.VMEM((per, G, most, *coded), BF16),
+            pltpu.VMEM((per, most, *piece), F32),
             DMA((4,)), DMA, DMA((R, KP)), DMA((2, C - 1)), DMA((R + 1, SP)),
-            DMA((R, BP)), DMA((C - 1, per, BP)), DMA((per, G - 1, BP)), DMA,
+            DMA((R, most)), DMA((C - 1, per, most)), DMA((per, G - 1, most)), DMA,
         ],
         compiler_params=pltpu.CompilerParams(
             collective_id=0, has_side_effects=True, vmem_limit_bytes=28 * 1024 * 1024),

time: 27.9 us -> 26.9 us (0.964)
  Pallas kernels: 26.9 us -> 26 us
    pallas_call x1, Pallas kernels: 25.9 us -> 24.9 us  [body(): pl.pallas_call(functools.partial(kernel, sizes), out_shape=(jax.ShapeDtyp...]
where the time goes in v5:
time: 26.9 us; the launch traced here: 26.8 us
  Pallas kernels  26 us (97%)
  between operations  0.82 us (3%)
    pallas_call x1, Pallas kernels, body(): pl.pallas_call(functools.partial(kernel, sizes), out_shape=(jax.ShapeDtyp...  24.9 us
    pallas_call x1, Pallas kernels, body(): pl.pallas_call(store, out_shape=(jax.ShapeDtypeStruct((rows, db), F32), j...  1.05 us

profile of v5, /device:TPU:3, one launch (start us, length us, event | category | flops | bytes accessed | tf_op | source)
XLA Modules:
  0.0 26.8 jit_solution(13983660297545213261)
XLA Ops:
  0.6 24.9 %shard_map.59 = (f32[128,1536]{1,0:T(8,128)S(1)}, f32[64,1024]{1,0:T(8,128)S(1)}) custom-call(bf16[12,8,128,128]{3,2,1,0:T(8,128)(2,1)} %eri.1, s32[8,12]{1,0:T(8,128)} %bitcast.4, bf16[1536,128]{1,0:T(8,128)(2,1)} %dbra.1, bf16[64,1024]{1,0:T(8,128)(2,1)} %bitcast.3), custom_call_target="tpu_custom_call" | custom-call | tf_op jit(solution)/shard_map/pallas_call | solution.py:410
  25.5 1.0 %shard_map.60 = (f32[1536,128]{1,0:T(8,128)}, f32[64,1024]{1,0:T(8,128)}) custom-call(f32[128,1536]{1,0:T(8,128)S(1)} %get-tuple-element.6.bra_t, f32[64,1024]{1,0:T(8,128)S(1)} %get-tuple-element.7.ket_t), custom_call_target="tpu_custom_call" | custom-call | tf_op jit(solution)/shard_map/pallas_call | solution.py:436

commit v6 on v5

--- a/solution.py
+++ b/solution.py
@@ -11,6 +11,7 @@
 F32 = jnp.float32
 BF16 = jnp.bfloat16
 STEPS = 7 * 2.0**8
+TINY = 1e-36
 KP = 4
 SP = 4
 HOPS = (6, 4)
@@ -23,7 +24,7 @@
     w = v.shape[1]
     top = v.astype(BF16)
     near = top.astype(F32)
-    rest = jnp.round((v - near) / jnp.where(near == 0, 1.0, near) * STEPS)
+    rest = jnp.round((v - near) / jnp.where(jnp.abs(near) < TINY, 1.0, near) * STEPS)
     ref[:, :w] = top
     ref[:, w:] = (rest[:, :w // 2] * 16 + rest[:, w // 2:]).astype(BF16)
 

time: 26.9 us -> 26.9 us (level)
  no operation moved by 1% of the time
where the time goes in v6:
time: 26.9 us; the launch traced here: 26.8 us
  Pallas kernels  26 us (97%)
  between operations  0.82 us (3%)
    pallas_call x1, Pallas kernels, body(): pl.pallas_call(functools.partial(kernel, sizes), out_shape=(jax.ShapeDtyp...  24.9 us
    pallas_call x1, Pallas kernels, body(): pl.pallas_call(store, out_shape=(jax.ShapeDtypeStruct((rows, db), F32), j...  1.05 us

profile of v6, /device:TPU:3, one launch (start us, length us, event | category | flops | bytes accessed | tf_op | source)
XLA Modules:
  0.0 26.8 jit_solution(7895539529476590575)
XLA Ops:
  0.6 24.9 %shard_map.59 = (f32[128,1536]{1,0:T(8,128)S(1)}, f32[64,1024]{1,0:T(8,128)S(1)}) custom-call(bf16[12,8,128,128]{3,2,1,0:T(8,128)(2,1)} %eri.1, s32[8,12]{1,0:T(8,128)} %bitcast.4, bf16[1536,128]{1,0:T(8,128)(2,1)} %dbra.1, bf16[64,1024]{1,0:T(8,128)(2,1)} %bitcast.3), custom_call_target="tpu_custom_call" | custom-call | tf_op jit(solution)/shard_map/pallas_call | solution.py:411
  25.5 1.0 %shard_map.60 = (f32[1536,128]{1,0:T(8,128)}, f32[64,1024]{1,0:T(8,128)}) custom-call(f32[128,1536]{1,0:T(8,128)S(1)} %get-tuple-element.6.bra_t, f32[64,1024]{1,0:T(8,128)S(1)} %get-tuple-element.7.ket_t), custom_call_target="tpu_custom_call" | custom-call | tf_op jit(solution)/shard_map/pallas_call | solution.py:437
